TPU v7x, 256 devices: a 2x2x32 block of a 4x8x32 slice. The times are simulated.
256 devices in a mesh: grp: 4 (over y, x), seq: 32 (over z), tp: 2 (over core).
Axes of the slice: x: 2, y: 2, z: 32, core: 2. Of those that a mesh axis runs over, the one named last changes fastest.
The devices are a block of a 4x8x32 slice.
Arguments:
- visual_q: bfloat16 [32768, 1536], P(('grp', 'seq'), 'tp'), parts along dimension 0, may hold values from -8 to 8
- visual_key_input: bfloat16 [32768, 1536], P(('grp', 'seq'), 'tp'), parts along dimension 0, may hold values from -8 to 8
- visual_v: bfloat16 [32768, 1536], P(('grp', 'seq'), 'tp'), parts along dimension 0, may hold values from -6 to 6
- text_k: bfloat16 [1024, 1536], P(('grp', 'seq'), 'tp'), parts along dimension 0, may hold values from -6 to 6
- text_v: bfloat16 [1024, 1536], P(('grp', 'seq'), 'tp'), parts along dimension 0, may hold values from -6 to 6
- text_mask: int32 [1024], P(('grp', 'seq')), parts along dimension 0, may hold values from 0 to 1, as said below
- slab_order: int32 [128], P(('grp', 'seq')), parts along dimension 0, may hold values from 0 to 31, each once
- q_gain: float32 [128], replicated, may hold values from 0.8 to 6
- key_norm_gain: float32 [128], replicated, may hold values from 0.8 to 6
- w_out: bfloat16 [1536, 3072], P('tp'), may hold values from -0.8984375 to 0.8984375
Outputs:
- attended: bfloat16 [32768, 3072], P(('grp', 'seq', 'tp')), parts along dimension 0
There are 4 independent parts, one for each index of `grp`. A program takes and returns all parts, laid end to end along the dimension named above; an argument that names none is the same for every part. Nothing has to cross between parts.
Inputs may be any that keep to these rules, and one draw needn't show every extreme that they name: `text_mask`: the first entries are 1 and the rest 0, with at least 32 ones. `slab_order`: each slab number once.
All inputs are finite; a program needn't handle non-finite values.
Results may differ from a plain program's by a relative error of at most 0.013.
The roundings to bfloat16 on the way count: a program that leaves them out, or rounds other values in their place, can miss the bound.
Values may be sent and summed in bfloat16 or wider, within the bound.
No kernel may reach another device: no remote copies, remote signals or barrier semaphores. Data moves between devices by JAX's collectives and lax.ppermute only.
A program may use at most 128 MiB of HBM per device.

v0:
```python
import jax
import jax.numpy as jnp
from jax import lax
from jax.sharding import PartitionSpec as P

PARTS = 4
SLAB_H = 2
WIDE = 32
PARTS = (32, 48, 48)
NEGATIVE = -1e30


def from_everyone(shard, axis):
    size = lax.axis_size(axis)
    return lax.all_to_all(
        jnp.broadcast_to(shard[None], (size, *shard.shape)), axis, 0, 0, tiled=True
    )


def of_everyone(shard, axis):
    return from_everyone(shard, axis).astype(jnp.float32).sum(axis=0)


def apply_norm(x, gain):
    x32 = x.astype(jnp.float32).reshape(x.shape[0], -1, 128)
    scale = lax.rsqrt(jnp.mean(x32 * x32, axis=-1, keepdims=True) + 0.05)
    return x32 * scale * gain


def angles(frame, height, column):
    pieces = []
    for pos, size in zip((frame, height, column), PARTS):
        half = size // 2
        freq = 10000.0 ** (-jnp.arange(half, dtype=jnp.float32) / half)
        pieces.append(pos.astype(jnp.float32)[:, None] * freq[None, :])
    angle = jnp.concatenate(pieces, axis=-1)
    return (jnp.cos(angle), jnp.sin(angle))


def apply_rotation(x, cosine_table, sine_table):
    outs = []
    offset = 0
    column = 0
    for size in PARTS:
        half = size // 2
        first = x[..., offset : offset + half]
        second = x[..., offset + half : offset + size]
        cpart = cosine_table[:, None, column : column + half]
        spart = sine_table[:, None, column : column + half]
        outs.append(first * cpart - second * spart)
        outs.append(second * cpart + first * spart)
        offset += size
        column += half
    return jnp.concatenate(outs, axis=-1)


def block_rows(count):
    for candidate in range(2048, 255, -1):
        if count % candidate == 0:
            return candidate
    return count


def absorb(carry, queries, key_rows, values, marks):
    count = key_rows.shape[0]
    heads = queries.shape[1]
    step_rows = block_rows(count)

    def update(state, block):
        key_block, value_block, mark_block = block
        top, total, accum = state
        scores = jnp.einsum(
            "qhd,khd->qhk",
            queries,
            key_block.reshape(-1, heads, 128),
            preferred_element_type=jnp.float32,
        )
        scores = scores + mark_block.astype(jnp.float32)[None, None, :]
        fresh_top = jnp.maximum(top, jnp.max(scores, axis=-1))
        probs = jnp.exp(scores - fresh_top[..., None])
        factor = jnp.exp(top - fresh_top)
        total = total * factor + jnp.sum(probs, axis=-1)
        mixed = jnp.einsum(
            "qhk,khd->qhd",
            probs.astype(jnp.bfloat16),
            value_block.reshape(-1, heads, 128),
            preferred_element_type=jnp.float32,
        )
        accum = accum * factor[..., None] + mixed
        return ((fresh_top, total, accum), None)

    if step_rows == count:
        return update(carry, (key_rows, values, marks))[0]
    turns = count // step_rows
    blocks = (
        key_rows.reshape(turns, step_rows, -1),
        values.reshape(turns, step_rows, -1),
        marks.reshape(turns, step_rows),
    )
    return lax.scan(update, carry, blocks)[0]


def body(
    visual_q,
    visual_key_input,
    visual_v,
    text_k,
    text_v,
    text_mask,
    slab_order,
    q_gain,
    key_norm_gain,
    w_out,
):
    rows = visual_q.shape[0]
    width = visual_q.shape[1]
    heads = width // 128
    local = jnp.arange(rows, dtype=jnp.int32)
    frame = local // (SLAB_H * WIDE)
    height = slab_order[0] * SLAB_H + local // WIDE % SLAB_H
    column = local % WIDE
    cosine_table, sine_table = angles(frame, height, column)
    queries = (
        apply_rotation(apply_norm(visual_q, q_gain), cosine_table, sine_table)
        / jnp.sqrt(jnp.float32(128))
    ).astype(jnp.bfloat16)
    visual_key_rows = (
        apply_rotation(apply_norm(visual_key_input, key_norm_gain), cosine_table, sine_table)
        .astype(jnp.bfloat16)
        .reshape(rows, width)
    )
    textual_keys = (
        apply_norm(text_k, key_norm_gain).astype(jnp.bfloat16).reshape(text_k.shape[0], width)
    )
    text_marks = jnp.where(text_mask == 1, 0.0, NEGATIVE).astype(jnp.bfloat16)
    start_state = (
        jnp.full((rows, heads), NEGATIVE, jnp.float32),
        jnp.zeros((rows, heads), jnp.float32),
        jnp.zeros((rows, heads, 128), jnp.float32),
    )
    joint_keys = jnp.concatenate([visual_key_rows, textual_keys], axis=0)
    joint_values = jnp.concatenate([visual_v, text_v], axis=0)
    joint_marks = jnp.concatenate([jnp.zeros((rows,), jnp.bfloat16), text_marks], axis=0)
    state = absorb(
        start_state,
        queries,
        lax.all_gather(joint_keys, "seq", axis=0, tiled=True),
        lax.all_gather(joint_values, "seq", axis=0, tiled=True),
        lax.all_gather(joint_marks, "seq", axis=0, tiled=True),
    )
    top, total, accum = state
    heads_out = (accum / total[..., None]).astype(jnp.bfloat16).reshape(rows, width)
    share = rows // lax.axis_size("tp")
    summed = of_everyone(
        jnp.dot(heads_out, w_out, preferred_element_type=jnp.float32).astype(jnp.bfloat16), "tp"
    ).astype(jnp.float32)
    kept = lax.dynamic_slice_in_dim(summed, lax.axis_index("tp") * share, share, 0)
    return kept.astype(jnp.bfloat16)


def solution(mesh):
    placed = (
        P(("grp", "seq"), "tp"),
        P(("grp", "seq"), "tp"),
        P(("grp", "seq"), "tp"),
        P(("grp", "seq"), "tp"),
        P(("grp", "seq"), "tp"),
        P(("grp", "seq")),
        P(("grp", "seq")),
        P(),
        P(),
        P("tp", None),
    )
    return jax.shard_map(
        body, mesh=mesh, in_specs=placed, out_specs=P(("grp", "seq", "tp"), None), check_vma=False
    )
```

profile of v0, /device:TPU:37, one launch (start us, length us, event | category | flops | bytes accessed | tf_op | source)
XLA Modules:
  0.0 474.0 jit_solution(3188589150645841553)
XLA Ops:
  16.3 113.2 %all-reduce.1 = bf16[8448]{0:T(1024)(128)(2,1)S(1)} all-reduce(bf16[8448]{0:T(1024)(128)(2,1)S(1)} %dynamic-update-slice), channel_id=1, replica_groups=mesh['grp'=4,'seq'=32,'tp'=2] {'seq'}, use_global_device_ids=true, to_apply=%add.1 | all-reduce | flops 8448 | bytes 33792
  130.5 58.8 %all-gather.3.cloned.1.call-done = bf16[8448,768]{1,0:T(8,128)(2,1)} async-done(((bf16[264,768]{1,0:T(8,128)(2,1)}), bf16[8448,768]{1,0:T(8,128)(2,1)}) %all-gather.3.cloned.1.call-update) | async-done | bytes 12976144 | tf_op jit(solution)/shard_map/all_gather | solution.py:147
  189.3 162.7 %all-gather.5.cloned.1.call-done = bf16[8448,768]{1,0:T(8,128)(2,1)} async-done(((bf16[264,768]{1,0:T(8,128)(2,1)}), bf16[8448,768]{1,0:T(8,128)(2,1)}) %all-gather.5.cloned.1.call-update) | async-done | bytes 12976144 | tf_op jit(solution)/shard_map/all_gather | solution.py:148
  352.0 98.3 %while.15 = (s32[]{:T(128)}, f32[256,6]{0,1:T(8,128)S(1)}, f32[256,6]{0,1:T(8,128)S(1)}, f32[256,6,128]{0,2,1:T(8,128)S(1)}, bf16[6,1408,768]{2,1,0:T(8,128)(2,1...) while((s32[]{:T(128)}, f32[256,6]{0,1:T(8,128)S(1)}, ...), condition=%wide.region_6.7_spmd.clone, body=%wide.region_3.6_spmd.clone.sunk | while | flops 1125196672 | bytes 49668988 | solution.py:100
  352.0 3.9 constant_dynamic-slice_fusion.3
  358.4 2.9 copy.63
  361.3 3.1 bitcast_reduce_fusion.2
  368.4 3.9 constant_dynamic-slice_fusion.3
  374.8 2.9 copy.63
  377.7 3.1 bitcast_reduce_fusion.2
  384.8 3.9 constant_dynamic-slice_fusion.3
  391.1 2.9 copy.63
  394.1 3.1 bitcast_reduce_fusion.2
  401.2 3.9 constant_dynamic-slice_fusion.3
  407.5 2.9 copy.63
  410.4 3.1 bitcast_reduce_fusion.2
  417.6 3.9 constant_dynamic-slice_fusion.3
  423.9 2.9 copy.63
  426.8 3.1 bitcast_reduce_fusion.2
  433.9 3.9 constant_dynamic-slice_fusion.3
  440.3 2.9 copy.63
  443.2 3.1 bitcast_reduce_fusion.2
  450.4 3.8 convolution_convert_fusion
  454.5 11.1 %all_to_all.5 = bf16[2,256,3072]{2,1,0:T(8,128)(2,1)S(1)} all-to-all(bf16[2,256,3072]{2,1,0:T(8,128)(2,1)S(1)} %broadcast_in_dim.19), channel_id=1, replica_groups=mesh['grp'=4,'seq'=32,'tp'=2] {'tp'}, dimensions={0} | all-to-all | bytes 6291456 | tf_op jit(solution)/shard_map/all_to_all | solution.py:15
  (112 shorter events, 49.0 us)
Async XLA Ops:
  6.5 8.1 %copy-start.5 = (u32[256]{0:T(256)S(1)}, u32[256]{0:T(256)}, u32[]{:S(2)}) copy-start(u32[256]{0:T(256)} %constant.118) | copy-start | bytes 3076
  6.5 7.2 %copy-start.2 = (bf16[8,768]{1,0:T(8,128)(2,1)S(1)}, bf16[8,768]{1,0:T(8,128)(2,1)}, u32[]{:S(2)}) copy-start(bf16[8,768]{1,0:T(8,128)(2,1)} %param.16) | copy-start | bytes 36868
  6.6 7.2 %copy-start = (bf16[256,768]{1,0:T(8,128)(2,1)S(1)}, bf16[256,768]{1,0:T(8,128)(2,1)}, u32[]{:S(2)}) copy-start(bf16[256,768]{1,0:T(8,128)(2,1)} %param.14) | copy-start | bytes 1179652
  6.6 9.5 %copy-start.4 = (s32[8]{0:T(128)S(1)}, s32[8]{0:T(128)}, u32[]{:S(2)}) copy-start(s32[8]{0:T(128)} %param.17) | copy-start | bytes 100
  6.6 123.0 %copy-start.1 = (bf16[256,768]{1,0:T(8,128)(2,1)S(1)}, bf16[256,768]{1,0:T(8,128)(2,1)}, u32[]{:S(2)}) copy-start(bf16[256,768]{1,0:T(8,128)(2,1)} %param.12) | copy-start | bytes 1179652
  6.6 182.8 %all-gather.3.cloned.1.call-start = ((), (), s32[]{:S(2)}) async-start(), calls=%async_computation.1 | async-start | bytes 13381632 | tf_op jit(solution)/shard_map/all_gather | solution.py:147
  10.2 119.6 %copy-start.3 = (f32[128]{0:T(128)S(1)}, f32[128]{0:T(128)}, u32[]{:S(2)}) copy-start(f32[128]{0:T(128)} %param.19) | copy-start | bytes 1540
  13.6 338.4 %all-gather.5.cloned.1.call-start = ((), (), s32[]{:S(2)}) async-start(), calls=%async_computation.2 | async-start | bytes 13381632 | tf_op jit(solution)/shard_map/all_gather | solution.py:148
Sparse Core Ops, SparseCore 0:
  13.7 175.5 all-gather.2
  191.1 160.8 all-gather.4
where the time goes:
time: 475 us; the launch traced here: 474 us
  waiting for transfers between devices  222 us (47%)
  blocking collectives  124 us (26%)
  local copies, waits for them, and re-layouts  61.2 us (13%)
  matrix products  34.7 us (7%)
  other arithmetic  16.4 us (3%)
  between operations  15.2 us (3%)
    all_gather x1, waiting for transfers between devices, body(): lax.all_gather(joint_values, 'seq', axis=0, tiled=True)  163 us
    unnamed x1, blocking collectives  113 us
    all_gather x1, waiting for transfers between devices, body(): lax.all_gather(joint_keys, 'seq', axis=0, tiled=True)  58.8 us
    dynamic_slice x18, local copies, waits for them, and re-layouts, absorb(): return lax.scan(update, carry, blocks)[0]  55.4 us
    dot_general x6, matrix products, update(): jnp.einsum('qhd,khd->qhk', queries, key_block.reshape(-1, heads, 128), pr...  18.8 us
    dot_general x6, matrix products, update(): jnp.einsum('qhk,khd->qhd', probs.astype(jnp.bfloat16), value_block.reshap...  12.1 us
    reduce_sum x6, other arithmetic, update(): total = total * factor + jnp.sum(probs, axis=-1)  11.1 us
    all_to_all x1, blocking collectives, from_everyone(): lax.all_to_all(jnp.broadcast_to(shard[None], (size, *shard.shape)), axis,...  11.1 us
  transfers between devices with their start and end apart: 2, of which 2 were waited for; matrix products, arithmetic and copies ran while one was open for 1% of the time, Pallas kernels for 0%

commit v1 on v0

--- a/solution.py
+++ b/solution.py
@@ -8,6 +8,12 @@
 WIDE = 32
 PARTS = (32, 48, 48)
 NEGATIVE = -1e30
+
+
+def gather_by_exchange(x, axis, dim):
+    devices = lax.axis_size(axis)
+    repeats = [devices if d == dim else 1 for d in range(x.ndim)]
+    return lax.all_to_all(jnp.tile(x, repeats), axis, split_axis=dim, concat_axis=dim, tiled=True)
 
 
 def from_everyone(shard, axis):
@@ -145,7 +151,7 @@
         start_state,
         queries,
         lax.all_gather(joint_keys, "seq", axis=0, tiled=True),
-        lax.all_gather(joint_values, "seq", axis=0, tiled=True),
+        gather_by_exchange(joint_values, "seq", 0),
         lax.all_gather(joint_marks, "seq", axis=0, tiled=True),
     )
     top, total, accum = state

time: 475 us -> 1510 us (3.18)
  blocking collectives: 124 us -> 1340 us
  waiting for transfers between devices: 222 us -> 0.08 us
  starting transfers between devices: 0.13 us -> 33.4 us
    unnamed x1, blocking collectives: 113 us -> 1310 us
    all_gather x1 -> x0, waiting for transfers between devices: 163 us -> none  [body(): lax.all_gather(joint_values, 'seq', axis=0, tiled=True)]
    all_gather x1, waiting for transfers between devices: 58.8 us -> 0.02 us  [body(): lax.all_gather(joint_keys, 'seq', axis=0, tiled=True)]
    all_to_all x0 -> x1, starting transfers between devices: none -> 33.3 us  [gather_by_exchange(): lax.all_to_all(jnp.tile(x, repeats), axis, split_axis=dim, concat_axis=di...]
    all_to_all x1, blocking collectives: 11.1 us -> 30.4 us  [from_everyone(): lax.all_to_all(jnp.broadcast_to(shard[None], (size, *shard.shape)), axis,...]
  transfers between devices with their start and end apart: 2 -> 2, of which waited for: 2 -> 0; matrix products, arithmetic and copies ran while one was open for 1% -> 0% of each run, Pallas kernels for 0% -> 0%
where the time goes in v1:
time: 1510 us
  blocking collectives  1340 us (89%)
  local copies, waits for them, and re-layouts  65.1 us (4%)
  matrix products  34.7 us (2%)
  starting transfers between devices  33.4 us (2%)
  between operations  15.2 us (1%)
    unnamed x1, blocking collectives  1310 us
    dynamic_slice x18, local copies, waits for them, and re-layouts, absorb(): return lax.scan(update, carry, blocks)[0]  55.4 us
    all_to_all x1, starting transfers between devices, gather_by_exchange(): lax.all_to_all(jnp.tile(x, repeats), axis, split_axis=dim, concat_axis=di...  33.3 us
    all_to_all x1, blocking collectives, from_everyone(): lax.all_to_all(jnp.broadcast_to(shard[None], (size, *shard.shape)), axis,...  30.4 us
  transfers between devices with their start and end apart: 2, of which 0 were waited for; matrix products, arithmetic and copies ran while one was open for 0% of the time, Pallas kernels for 0%

profile of v1, /device:TPU:37, one launch (start us, length us, event | category | flops | bytes accessed | tf_op | source)
XLA Modules:
  0.0 1505.6 jit_solution(4993421953843216129)
XLA Ops:
  7.6 5.5 tile.2
  13.1 33.3 %all-to-all-start = ((bf16[32,264,768]{2,1,0:T(8,128)(2,1)}), bf16[32,264,768]{2,1,0:T(8,128)(2,1)}, u32[]{:S(2)}, u32[]{:S(2)}) async-start(bf16[32,264,768]{2,1,0:T(8,128)(2,1)} %tile.2), calls=%async_computation | async-start | bytes 25952256 | tf_op jit(solution)/shard_map/all_to_all | solution.py:16
  51.6 1311.7 %all-reduce.1 = bf16[8448]{0:T(1024)(128)(2,1)S(1)} all-reduce(bf16[8448]{0:T(1024)(128)(2,1)S(1)} %dynamic-update-slice), channel_id=1, replica_groups=mesh['grp'=4,'seq'=32,'tp'=2] {'seq'}, use_global_device_ids=true, to_apply=%add.1 | all-reduce | flops 8448 | bytes 33792
  1364.3 98.3 %while.15 = (s32[]{:T(128)}, f32[256,6]{0,1:T(8,128)S(1)}, f32[256,6]{0,1:T(8,128)S(1)}, f32[256,6,128]{0,2,1:T(8,128)S(1)}, bf16[6,1408,768]{2,1,0:T(8,128)(2,1...) while((s32[]{:T(128)}, f32[256,6]{0,1:T(8,128)S(1)}, ...), condition=%wide.region_6.7_spmd.clone, body=%wide.region_3.6_spmd.clone.sunk | while | flops 1125196672 | bytes 49668988 | solution.py:106
  1364.4 3.9 constant_dynamic-slice_fusion.3
  1370.7 2.9 copy.63
  1373.6 3.1 bitcast_reduce_fusion.2
  1380.7 3.9 constant_dynamic-slice_fusion.3
  1387.1 2.9 copy.63
  1390.0 3.1 bitcast_reduce_fusion.2
  1397.1 3.9 constant_dynamic-slice_fusion.3
  1403.5 2.9 copy.63
  1406.4 3.1 bitcast_reduce_fusion.2
  1413.5 3.9 constant_dynamic-slice_fusion.3
  1419.8 2.9 copy.63
  1422.8 3.1 bitcast_reduce_fusion.2
  1429.9 3.9 constant_dynamic-slice_fusion.3
  1436.2 2.9 copy.63
  1439.1 3.1 bitcast_reduce_fusion.2
  1446.3 3.9 constant_dynamic-slice_fusion.3
  1452.6 2.9 copy.63
  1455.5 3.1 bitcast_reduce_fusion.2
  1462.7 3.8 convolution_convert_fusion
  1466.8 30.4 %all_to_all.11 = bf16[2,256,3072]{2,1,0:T(8,128)(2,1)S(1)} all-to-all(bf16[2,256,3072]{2,1,0:T(8,128)(2,1)S(1)} %broadcast_in_dim.19), channel_id=1, replica_groups=mesh['grp'=4,'seq'=32,'tp'=2] {'tp'}, dimensions={0} | all-to-all | bytes 6291456 | tf_op jit(solution)/shard_map/all_to_all | solution.py:21
  (114 shorter events, 45.5 us)
Async XLA Ops:
  13.1 34.7 %copy-start.2 = (bf16[8,768]{1,0:T(8,128)(2,1)S(1)}, bf16[8,768]{1,0:T(8,128)(2,1)}, u32[]{:S(2)}) copy-start(bf16[8,768]{1,0:T(8,128)(2,1)} %param.15) | copy-start | bytes 36868
  13.1 34.7 %copy-start.3 = (f32[128]{0:T(128)S(1)}, f32[128]{0:T(128)}, u32[]{:S(2)}) copy-start(f32[128]{0:T(128)} %param.20) | copy-start | bytes 1540
  13.1 35.0 %copy-start = (bf16[256,768]{1,0:T(8,128)(2,1)S(1)}, bf16[256,768]{1,0:T(8,128)(2,1)}, u32[]{:S(2)}) copy-start(bf16[256,768]{1,0:T(8,128)(2,1)} %param.13) | copy-start | bytes 1179652
  13.1 1351.2 %all-to-all-start = ((bf16[32,264,768]{2,1,0:T(8,128)(2,1)}), bf16[32,264,768]{2,1,0:T(8,128)(2,1)}, u32[]{:S(2)}, u32[]{:S(2)}) async-start(bf16[32,264,768]{2,1,0:T(8,128)(2,1)} %tile.2), calls=%async_computation | async-start | bytes 25952256 | tf_op jit(solution)/shard_map/all_to_all | solution.py:16
  46.5 3.4 copy-start.6
  46.5 4.8 copy-start.5
  46.5 1316.8 %copy-start.1 = (bf16[256,768]{1,0:T(8,128)(2,1)S(1)}, bf16[256,768]{1,0:T(8,128)(2,1)}, u32[]{:S(2)}) copy-start(bf16[256,768]{1,0:T(8,128)(2,1)} %param.12) | copy-start | bytes 1179652
  46.5 1317.1 %copy-start.4 = (f32[128]{0:T(128)S(1)}, f32[128]{0:T(128)}, u32[]{:S(2)}) copy-start(f32[128]{0:T(128)} %param.19) | copy-start | bytes 1540
  46.5 1317.7 %all-gather.2.cloned.1.call-start = ((), (), s32[]{:S(2)}) async-start(), calls=%async_computation.2 | async-start | bytes 13381632 | tf_op jit(solution)/shard_map/all_gather | solution.py:153
Sparse Core Ops, SparseCore 0:
  50.0 1249.1 all-gather.1
